TPU v7x, 32 devices: a whole 2x2x4 slice. The times are simulated.
32 devices in a mesh: row: 4 (over y, x), col: 8 (over z, core).
Axes of the slice: x: 2, y: 2, z: 4, core: 2. Of those that a mesh axis runs over, the one named last changes fastest.
Arguments:
- left_matrix: float32 [4096, 4096], P('row', 'col'), may hold values from -6 to 6
- right_matrix: float32 [4096, 4096], P('row', 'col'), may hold values from -0.09375 to 0.09375
Outputs:
- product_matrix: float32 [4096, 4096], P('row', 'col')
All inputs are finite; a program needn't handle non-finite values.
Results may differ from a plain program's by a relative error of at most 0.00019.
Values sent between devices are 32-bit elements; how exact they have to be, the bound alone decides.
A program may use at most 64 MiB of HBM per device.

v0:
```python
import jax
import jax.numpy as jnp
from jax import lax
from jax.sharding import PartitionSpec as P


def multiply(left_term, right_term):
    return jnp.dot(
        left_term, right_term, precision=lax.Precision.HIGHEST, preferred_element_type=jnp.float32
    )


def body(left_matrix, right_matrix):
    row_panel = lax.all_gather(left_matrix, "col", axis=1, tiled=True)
    col_panel = lax.all_gather(right_matrix, "row", axis=0, tiled=True)
    return multiply(row_panel, col_panel)


def solution(mesh):
    placed = (P("row", "col"), P("row", "col"))
    return jax.shard_map(
        body, mesh=mesh, in_specs=placed, out_specs=P("row", "col"), check_vma=False
    )
```

profile of v0, /device:TPU:0, one launch (start us, length us, event | category | flops | bytes accessed | tf_op | source)
XLA Modules:
  0.0 289.9 jit_solution(7672909341723281923)
XLA Ops:
  6.5 0.0 all-gather.5.cloned.1.call-start
  6.5 0.7 all-gather.5.cloned.1.call-update
  7.3 0.0 all-gather.3.cloned.1.call-start
  7.3 0.7 all-gather.3.cloned.1.call-update
  8.0 91.4 %all-gather.5.cloned.1.call-done = f32[4096,512]{1,0:T(8,128)} async-done(((f32[1024,512]{1,0:T(8,128)}), f32[4096,512]{1,0:T(8,128)}) %all-gather.5.cloned.1.call-update) | async-done | bytes 8388624 | tf_op jit(solution)/shard_map/all_gather | solution.py:15
  99.4 152.7 %all-gather.3.cloned.1.call-done = f32[1024,4096]{1,0:T(8,128)} async-done(((f32[1024,512]{1,0:T(8,128)}), f32[1024,4096]{1,0:T(8,128)}) %all-gather.3.cloned.1.call-update) | async-done | bytes 16777232 | tf_op jit(solution)/shard_map/all_gather | solution.py:14
  252.1 31.0 %fusion = f32[1024,512]{1,0:T(8,128)} fusion(f32[1024,4096]{1,0:T(8,128)} %all-gather.3.cloned.1.call-done, f32[4096,512]{1,0:T(8,128)} %all-gather.5.cloned.1.call-done), kind=kOutput, calls=%fused_computation | convolution fusion | flops 25769803776 | bytes 27262976 | tf_op jit(solution)/shard_map/dot_general | solution.py:8
Async XLA Ops:
  6.5 92.9 %all-gather.5.cloned.1.call-start = ((), (), s32[]{:S(2)}) async-start(), calls=%async_computation.1 | async-start | bytes 10485760 | tf_op jit(solution)/shard_map/all_gather | solution.py:15
  7.3 244.9 %all-gather.3.cloned.1.call-start = ((), (), s32[]{:S(2)}) async-start(), calls=%async_computation | async-start | bytes 18874368 | tf_op jit(solution)/shard_map/all_gather | solution.py:14
Sparse Core Ops, SparseCore 0:
  9.2 90.1 all-gather.4
  101.0 151.0 all-gather.2
where the time goes:
time: 290 us
  waiting for transfers between devices  246 us (85%)
  matrix products  31 us (11%)
  between operations  13.4 us (5%)
    all_gather x1, waiting for transfers between devices, body(): row_panel = lax.all_gather(left_matrix, 'col', axis=1, tiled=True)  153 us
    all_gather x1, waiting for transfers between devices, body(): col_panel = lax.all_gather(right_matrix, 'row', axis=0, tiled=True)  91.4 us
    dot_general x1, matrix products, multiply(): jnp.dot(left_term, right_term, precision=lax.Precision.HIGHEST, preferred...  31 us
  transfers between devices with their start and end apart: 2, of which 2 were waited for; matrix products, arithmetic and copies ran while one was open for 0% of the time, Pallas kernels for 0%

commit v1 on v0

v1 whole, which is shorter than its diff:
```python
import functools

import jax
import jax.numpy as jnp
from jax import lax
from jax.experimental import pallas as pl
from jax.experimental.pallas import tpu as pltpu
from jax.sharding import PartitionSpec as P

MESH = pl.DeviceIdType.MESH
CHUNKS = 4


def split(value):
    high = value.astype(jnp.bfloat16)
    low = (value - high.astype(jnp.float32)).astype(jnp.bfloat16)
    return high, low


def kernel(rows, cols, a_in, b_in, out, a_all, b_all, b_high, b_low,
           a_recv, a_send, b_recv, b_send, local):
    row = lax.axis_index("row")
    col = lax.axis_index("col")
    core = lax.rem(col, 2)
    chip = lax.div(col, 2)
    chips = cols // 2
    height, a_depth = a_in.shape
    b_depth = b_in.shape[0]
    per_b = b_depth // a_depth
    size = height // CHUNKS
    partner = chip * 2 + 1 - core

    def left_valid(distance):
        return chip >= distance

    def right_valid(distance):
        return chip + distance < chips

    def a_copy(kind, block, chunk, own):
        part = pl.ds(chunk * size, size)
        target = (col + 2, col - 2, partner)[kind]
        return pltpu.make_async_remote_copy(
            src_ref=a_in.at[part] if own else a_all.at[block, part],
            dst_ref=a_all.at[block, part],
            send_sem=a_send.at[kind, block, chunk],
            recv_sem=a_recv.at[block, chunk],
            device_id={"col": target}, device_id_type=MESH)

    def a_wait(block, chunk):
        a_copy(2, block, chunk, False).wait_recv()

    def b_copy(peer, source):
        return pltpu.make_async_remote_copy(
            src_ref=b_in, dst_ref=b_all.at[source],
            send_sem=b_send.at[peer], recv_sem=b_recv.at[source],
            device_id={"row": peer}, device_id_type=MESH)

    barrier = pltpu.get_barrier_semaphore()

    @pl.when(chip > 0)
    def _():
        pl.semaphore_signal(barrier, inc=1, device_id={"col": col - 2}, device_id_type=MESH)

    @pl.when(chip < chips - 1)
    def _():
        pl.semaphore_signal(barrier, inc=1, device_id={"col": col + 2}, device_id_type=MESH)

    pl.semaphore_signal(barrier, inc=1, device_id={"col": partner}, device_id_type=MESH)
    peers = [lax.rem(row + offset, rows) for offset in range(1, rows)]
    for peer in peers:
        pl.semaphore_signal(barrier, inc=1, device_id={"row": peer}, device_id_type=MESH)
    own_a = pltpu.make_async_copy(a_in, a_all.at[col], local.at[0])
    own_b = pltpu.make_async_copy(b_in, b_all.at[row], local.at[1])
    own_a.start()
    own_b.start()
    near = jnp.where(chip > 0, 1, 0) + jnp.where(chip < chips - 1, 1, 0)
    pl.semaphore_wait(barrier, rows + near)

    for chunk in range(CHUNKS):
        @pl.when(right_valid(1))
        def _():
            a_copy(0, col, chunk, True).start()

        @pl.when(left_valid(1))
        def _():
            a_copy(1, col, chunk, True).start()
    for peer in peers:
        b_copy(peer, row).start()
    for chunk in range(CHUNKS):
        a_copy(2, col, chunk, True).start()

    out[...] = jnp.zeros_like(out)
    own_a.wait()
    own_b.wait()

    def multiply(block, chunk):
        part = pl.ds(pl.multiple_of(chunk * size, size), size)
        source = lax.div(block, per_b)
        offset = pl.multiple_of(lax.rem(block, per_b) * a_depth, a_depth)
        depth = pl.ds(offset, a_depth)
        high, low = split(a_all[block, part, :])
        right_high = b_high[source, depth, :]
        right_low = b_low[source, depth, :]
        dot = functools.partial(jnp.dot, preferred_element_type=jnp.float32)
        out[part, :] += (dot(low, right_high) + dot(high, right_low)) + dot(high, right_high)

    def split_b(source):
        @pl.loop(0, b_depth // 128)
        def _(index):
            part = pl.ds(pl.multiple_of(index * 128, 128), 128)
            high, low = split(b_all[source, part, :])
            b_high[source, part, :] = high
            b_low[source, part, :] = low

    def multiply_block(block):
        @pl.loop(0, CHUNKS)
        def _(chunk):
            multiply(block, chunk)

    for distance in range(1, chips - 1):
        for chunk in range(CHUNKS):
            @pl.when(left_valid(distance))
            def _():
                block = col - 2 * distance
                a_wait(block, chunk)

                @pl.when(right_valid(1))
                def _():
                    a_copy(0, block, chunk, False).start()
                a_copy(2, block, chunk, False).start()

            @pl.when(right_valid(distance))
            def _():
                block = col + 2 * distance
                a_wait(block, chunk)

                @pl.when(left_valid(1))
                def _():
                    a_copy(1, block, chunk, False).start()
                a_copy(2, block, chunk, False).start()

    split_b(row)
    for peer in peers:
        b_copy(peer, peer).wait_recv()
        split_b(peer)

    for chunk in range(CHUNKS):
        a_wait(partner, chunk)
    multiply_block(col)
    multiply_block(partner)
    for distance in range(1, chips - 1):
        for valid, step in ((left_valid, -2), (right_valid, 2)):
            @pl.when(valid(distance))
            def _():
                for chunk in range(CHUNKS):
                    a_wait(partner + step * distance, chunk)
                multiply_block(col + step * distance)
                multiply_block(partner + step * distance)

    if chips > 1:
        for valid, step in ((left_valid, -2), (right_valid, 2)):
            @pl.when(valid(chips - 1))
            def _():
                block = col + step * (chips - 1)
                other = partner + step * (chips - 1)
                for chunk in range(CHUNKS):
                    a_wait(block, chunk)
                    a_copy(2, block, chunk, False).start()
                    multiply(block, chunk)
                    a_wait(other, chunk)
                    multiply(other, chunk)

    for peer in peers:
        b_copy(peer, row).wait_send()
    for chunk in range(CHUNKS):
        a_copy(2, col, chunk, True).wait_send()
        for distance in range(0, chips):
            @pl.when(left_valid(distance) & right_valid(1))
            def _():
                a_copy(0, col - 2 * distance, chunk, False).wait_send()

            @pl.when(right_valid(distance) & left_valid(1))
            def _():
                a_copy(1, col + 2 * distance, chunk, False).wait_send()
        for distance in range(1, chips):
            @pl.when(left_valid(distance))
            def _():
                a_copy(2, col - 2 * distance, chunk, False).wait_send()

            @pl.when(right_valid(distance))
            def _():
                a_copy(2, col + 2 * distance, chunk, False).wait_send()


def body(rows, cols, left_matrix, right_matrix):
    height, a_depth = left_matrix.shape
    b_depth, width = right_matrix.shape
    return pl.pallas_call(
        functools.partial(kernel, rows, cols),
        out_shape=jax.ShapeDtypeStruct((height, width), jnp.float32),
        in_specs=[pl.BlockSpec(memory_space=pl.ANY)] * 2,
        out_specs=pl.BlockSpec(memory_space=pltpu.VMEM),
        scratch_shapes=[
            pltpu.VMEM((cols, height, a_depth), jnp.float32),
            pltpu.VMEM((rows, b_depth, width), jnp.float32),
            pltpu.VMEM((rows, b_depth, width), jnp.bfloat16),
            pltpu.VMEM((rows, b_depth, width), jnp.bfloat16),
            pltpu.SemaphoreType.DMA((cols, CHUNKS)),
            pltpu.SemaphoreType.DMA((3, cols, CHUNKS)),
            pltpu.SemaphoreType.DMA((rows,)),
            pltpu.SemaphoreType.DMA((rows,)),
            pltpu.SemaphoreType.DMA((2,)),
        ],
        compiler_params=pltpu.CompilerParams(
            collective_id=0, has_side_effects=True, vmem_limit_bytes=56 * 2**20),
    )(left_matrix, right_matrix)


def solution(mesh):
    placed = (P("row", "col"), P("row", "col"))
    return jax.shard_map(
        functools.partial(body, mesh.shape["row"], mesh.shape["col"]),
        mesh=mesh, in_specs=placed, out_specs=P("row", "col"), check_vma=False
    )
```

time: 290 us -> 149 us (0.51)
  waiting for transfers between devices: 246 us -> 0 us
  Pallas kernels: 0 us -> 145 us
  matrix products: 31 us -> 0 us
  between operations: 13.4 us -> 0.01 us
  local copies, waits for them, and re-layouts: 0 us -> 3.08 us
    all_gather x2 -> x0, waiting for transfers between devices: 244 us -> none  [the longest x1 153 us: body(): row_panel = lax.all_gather(left_matrix, 'col', axis=1, tiled=True)]
    pallas_call x0 -> x1, Pallas kernels: none -> 145 us  [body(): pl.pallas_call(functools.partial(kernel, rows, cols), out_shape=jax.Shape...]
    dot_general x1 -> x0, matrix products: 31 us -> none  [multiply(): jnp.dot(left_term, right_term, precision=lax.Precision.HIGHEST, preferred...]
    unnamed x0 -> x1, local copies, waits for them, and re-layouts: none -> 3.08 us
  transfers between devices with their start and end apart: 2 -> 0, of which waited for: 2 -> 0; matrix products, arithmetic and copies ran while one was open for 0% -> 0% of each run, Pallas kernels for 0% -> 0%
where the time goes in v1:
time: 149 us; the launch traced here: 148 us
  Pallas kernels  145 us (97%)
  local copies, waits for them, and re-layouts  3.08 us (2%)
    pallas_call x1, Pallas kernels, body(): pl.pallas_call(functools.partial(kernel, rows, cols), out_shape=jax.Shape...  145 us
    unnamed x1, local copies, waits for them, and re-layouts  3.08 us

profile of v1, /device:TPU:0, one launch (start us, length us, event | category | flops | bytes accessed | tf_op | source)
XLA Modules:
  0.0 148.2 jit_solution(6883544624582740164)
XLA Ops:
  0.0 145.1 %shard_map.28 = f32[1024,512]{1,0:T(8,128)} custom-call(f32[1024,512]{1,0:T(8,128)} %a_in.1, f32[1024,512]{1,0:T(8,128)} %b_in.1), custom_call_target="tpu_custom_call" | custom-call | tf_op jit(solution)/shard_map/pallas_call | solution.py:198
  145.1 3.1 %copy.4 = f32[1024,512]{1,0:T(8,128)} copy(f32[1024,512]{1,0:T(8,128)} %shard_map.28) | data formatting | bytes 4194304

commit v2 on v1

--- a/solution.py
+++ b/solution.py
@@ -216,9 +216,311 @@
     )(left_matrix, right_matrix)
 
 
+STEPS = 8
+LAG = 2
+EARLY = 2
+
+
+def shared_kernel(a_in, b_in, out, a_all, b_all, b_high, b_low, c_all, c_high, c_low, partial,
+                  a_recv, a_send, b_recv, b_send, c_recv, c_send, p_recv, p_send, local):
+    row = lax.axis_index("row")
+    col = lax.axis_index("col")
+    core = lax.rem(col, 2)
+    chip = lax.div(col, 2)
+    partner = chip * 2 + 1 - core
+    side = lax.div(chip, 2)
+    y = lax.div(row, 2)
+    x = lax.rem(row, 2)
+    x_near = y * 2 + 1 - x
+    y_near = (1 - y) * 2 + x
+    far_corner = (1 - y) * 2 + 1 - x
+    other_side = 1 - side
+    end = 6 * side + core
+    middle = 2 + 2 * side + core
+    other_middle = 4 - 2 * side + core
+    other_end = 6 - 6 * side + core
+    swap = 1 - 2 * core
+    is_end = (chip == 0) | (chip == 3)
+    is_middle = (chip == 1) | (chip == 2)
+    height, a_depth = a_in.shape
+    b_depth = b_in.shape[0]
+    a_size = height // STEPS
+    b_size = b_depth // STEPS
+
+    def a_copy(kind, target, block, step, own=False):
+        part = pl.ds(step * a_size, a_size)
+        return pltpu.make_async_remote_copy(
+            src_ref=a_in.at[part] if own else a_all.at[block, part],
+            dst_ref=a_all.at[block, part],
+            send_sem=a_send.at[kind, block, step], recv_sem=a_recv.at[block, step],
+            device_id={"col": target}, device_id_type=MESH)
+
+    def a_wait(block, step):
+        a_copy(2, partner, block, step).wait_recv()
+
+    def b_copy(kind, target, source, step, own=False):
+        part = pl.ds(step * b_size, b_size)
+        return pltpu.make_async_remote_copy(
+            src_ref=b_in.at[part] if own else b_all.at[source, part],
+            dst_ref=b_all.at[source, part],
+            send_sem=b_send.at[kind, step], recv_sem=b_recv.at[source, step],
+            device_id={"row": target}, device_id_type=MESH)
+
+    def b_wait(source):
+        for step in range(STEPS):
+            b_copy(0, x_near, source, step).wait_recv()
+
+    def c_down(step, own):
+        part = pl.ds(step * b_size, b_size)
+        return pltpu.make_async_remote_copy(
+            src_ref=b_in.at[part] if own else b_all.at[y_near, part],
+            dst_ref=c_all.at[x, part],
+            send_sem=c_send.at[0, step], recv_sem=c_recv.at[x, step],
+            device_id={"col": middle}, device_id_type=MESH)
+
+    def c_across(slot, step):
+        part = pl.ds(step * b_size, b_size)
+        return pltpu.make_async_remote_copy(
+            src_ref=c_all.at[slot, part], dst_ref=c_all.at[slot, part],
+            send_sem=c_send.at[1, step], recv_sem=c_recv.at[slot, step],
+            device_id={"row": x_near}, device_id_type=MESH)
+
+    def p_copy(step):
+        part = pl.ds(step * a_size, a_size)
+        return pltpu.make_async_remote_copy(
+            src_ref=partial.at[part], dst_ref=partial.at[part],
+            send_sem=p_send.at[step], recv_sem=p_recv.at[step],
+            device_id={"col": end}, device_id_type=MESH)
+
+    def split_into(source, full, high_all, low_all):
+        @pl.loop(0, b_depth // 128)
+        def _(index):
+            part = pl.ds(pl.multiple_of(index * 128, 128), 128)
+            high, low = split(full[source, part, :])
+            high_all[source, part, :] = high
+            low_all[source, part, :] = low
+
+    dot = functools.partial(jnp.dot, preferred_element_type=jnp.float32)
+
+    def multiply(into, part, block, high_all, low_all, source, half):
+        depth = pl.ds(pl.multiple_of(half * a_depth, a_depth), a_depth)
+        high, low = split(a_all[block, part, :])
+        right_high = high_all[source, depth, :]
+        right_low = low_all[source, depth, :]
+        into[part, :] += (dot(low, right_high) + dot(high, right_low)) + dot(high, right_high)
+
+    def multiply_source(source):
+        @pl.loop(0, 8)
+        def _(index):
+            size = height // 4
+            part = pl.ds(pl.multiple_of(lax.rem(index, 4) * size, size), size)
+            half = lax.div(index, 4)
+            multiply(out, part, 2 * source + half, b_high, b_low, source, half)
+
+    barrier = pltpu.get_barrier_semaphore()
+
+    def greet(target):
+        pl.semaphore_signal(barrier, inc=1, device_id=target, device_id_type=MESH)
+
+    greet({"col": partner})
+    for peer in (x_near, y_near, far_corner):
+        greet({"row": peer})
+
+    @pl.when(is_end)
+    def _():
+        greet({"col": middle})
+
+    @pl.when(is_middle)
+    def _():
+        greet({"col": end})
+        greet({"col": other_middle})
+
+    own_a = pltpu.make_async_copy(a_in, a_all.at[col], local.at[0])
+    own_b = pltpu.make_async_copy(b_in, b_all.at[row], local.at[1])
+    own_a.start()
+    own_b.start()
+    pl.semaphore_wait(barrier, jnp.where(is_end, 5, 6))
+
+    @pl.when(is_end)
+    def _():
+        donor = y == other_side
+        keeper = y == side
+
+        @pl.when(donor)
+        def _():
+            for step in range(STEPS):
+                c_down(step, True).start()
+                b_copy(1, y_near, row, step, True).start()
+
+        @pl.when(keeper)
+        def _():
+            for step in range(STEPS):
+                b_copy(0, x_near, row, step, True).start()
+                b_copy(1, y_near, row, step, True).start()
+            for step in range(STEPS):
+                b_copy(2, far_corner, row, step, True).start()
+
+        for step in range(STEPS):
+            a_copy(2, partner, col, step, True).start()
+        out[...] = jnp.zeros_like(out)
+        own_a.wait()
+        own_b.wait()
+
+        @pl.when(keeper)
+        def _():
+            for step in range(STEPS):
+                b_copy(1, y_near, y_near, step).wait_recv()
+                c_down(step, False).start()
+
+        for step in range(STEPS):
+            a_copy(0, middle, col, step, True).start()
+        for step in range(STEPS):
+            a_wait(middle, step)
+            a_copy(2, partner, middle, step).start()
+
+        @pl.when(donor)
+        def _():
+            b_wait(y_near)
+            b_wait(far_corner)
+
+        @pl.when(keeper)
+        def _():
+            b_wait(x_near)
+
+        for step in range(STEPS):
+            a_wait(end + swap, step)
+            a_wait(middle + swap, step)
+        for index in range(2):
+            split_into(2 * side + index, b_all, b_high, b_low)
+            multiply_source(2 * side + index)
+        for step in range(STEPS):
+            part = pl.ds(step * a_size, a_size)
+            p_copy(step).wait_recv()
+            out[part, :] += partial[part, :]
+
+        @pl.when(donor)
+        def _():
+            for step in range(STEPS):
+                c_down(step, True).wait_send()
+                b_copy(1, y_near, row, step, True).wait_send()
+
+        @pl.when(keeper)
+        def _():
+            for step in range(STEPS):
+                for kind, peer in enumerate((x_near, y_near, far_corner)):
+                    b_copy(kind, peer, row, step, True).wait_send()
+                c_down(step, False).wait_send()
+        for step in range(STEPS):
+            a_copy(2, partner, col, step, True).wait_send()
+            a_copy(0, middle, col, step, True).wait_send()
+            a_copy(2, partner, middle, step).wait_send()
+
+    @pl.when(is_middle)
+    def _():
+        sent = []
+
+        def go(copy):
+            copy.start()
+            sent.append(copy)
+
+        for step in range(STEPS):
+            go(a_copy(1, end, col, step, True))
+            go(a_copy(0, other_middle, col, step, True))
+        for step in range(EARLY):
+            go(b_copy(0, x_near, row, step, True))
+        for step in range(STEPS):
+            go(b_copy(1, y_near, row, step, True))
+        for step in range(STEPS):
+            go(a_copy(2, partner, col, step, True))
+        out[...] = jnp.zeros_like(out)
+        partial[...] = jnp.zeros_like(partial)
+        own_a.wait()
+        own_b.wait()
+        split_into(row, b_all, b_high, b_low)
+
+        for step in range(STEPS):
+            c_across(x, step).wait_recv()
+            go(c_across(x, step))
+            a_wait(other_middle, step)
+            go(a_copy(2, partner, other_middle, step))
+        for step in range(EARLY, STEPS):
+            go(b_copy(0, x_near, row, step, True))
+        split_into(x, c_all, c_high, c_low)
+
+        for step in range(STEPS + LAG):
+            if step < STEPS:
+                a_wait(end, step)
+                go(a_copy(0, other_middle, end, step))
+                go(a_copy(2, partner, end, step))
+            if step < LAG:
+                continue
+            if step == LAG:
+                b_wait(y_near)
+                split_into(y_near, b_all, b_high, b_low)
+                for index in range(STEPS):
+                    c_across(1 - x, index).wait_recv()
+                split_into(1 - x, c_all, c_high, c_low)
+            late = step - LAG
+            part = pl.ds(late * a_size, a_size)
+            a_wait(other_end, late)
+            go(a_copy(2, partner, other_end, late))
+            for block in (middle, other_middle, end, other_end):
+                a_wait(block + swap, late)
+
+            @pl.loop(0, 4)
+            def _(index):
+                multiply(partial, part, 4 * other_side + index, c_high, c_low,
+                         lax.div(index, 2), lax.rem(index, 2))
+
+            @pl.loop(0, 4)
+            def _(index):
+                source = lax.div(index, 2) * 2 + x
+                half = lax.rem(index, 2)
+                multiply(out, part, 2 * source + half, b_high, b_low, source, half)
+
+            go(p_copy(late))
+            b_copy(0, x_near, x_near, late).wait_recv()
+            go(b_copy(2, y_near, x_near, late))
+
+        split_into(x_near, b_all, b_high, b_low)
+        multiply_source(x_near)
+        b_wait(far_corner)
+        split_into(far_corner, b_all, b_high, b_low)
+        multiply_source(far_corner)
+        for copy in sent:
+            copy.wait_send()
+
+
+def shared_body(left_matrix, right_matrix):
+    height, a_depth = left_matrix.shape
+    b_depth, width = right_matrix.shape
+    dma = pltpu.SemaphoreType.DMA
+    return pl.pallas_call(
+        shared_kernel,
+        out_shape=jax.ShapeDtypeStruct((height, width), jnp.float32),
+        in_specs=[pl.BlockSpec(memory_space=pl.ANY)] * 2,
+        out_specs=pl.BlockSpec(memory_space=pltpu.VMEM),
+        scratch_shapes=[
+            pltpu.VMEM((8, height, a_depth), jnp.float32),
+            pltpu.VMEM((4, b_depth, width), jnp.float32),
+            pltpu.VMEM((4, b_depth, width), jnp.bfloat16),
+            pltpu.VMEM((4, b_depth, width), jnp.bfloat16),
+            pltpu.VMEM((2, b_depth, width), jnp.float32),
+            pltpu.VMEM((2, b_depth, width), jnp.bfloat16),
+            pltpu.VMEM((2, b_depth, width), jnp.bfloat16),
+            pltpu.VMEM((height, width), jnp.float32),
+            dma((8, STEPS)), dma((3, 8, STEPS)), dma((4, STEPS)), dma((3, STEPS)),
+            dma((2, STEPS)), dma((2, STEPS)), dma((STEPS,)), dma((STEPS,)), dma((2,)),
+        ],
+        compiler_params=pltpu.CompilerParams(
+            collective_id=1, has_side_effects=True, vmem_limit_bytes=60 * 2**20),
+    )(left_matrix, right_matrix)
+
+
 def solution(mesh):
     placed = (P("row", "col"), P("row", "col"))
+    rows, cols = mesh.shape["row"], mesh.shape["col"]
+    part = shared_body if (rows, cols) == (4, 8) else functools.partial(body, rows, cols)
     return jax.shard_map(
-        functools.partial(body, mesh.shape["row"], mesh.shape["col"]),
-        mesh=mesh, in_specs=placed, out_specs=P("row", "col"), check_vma=False
+        part, mesh=mesh, in_specs=placed, out_specs=P("row", "col"), check_vma=False
     )

time: 149 us -> 140 us (0.940)
  the two profiles are of different devices: /device:TPU:0 before, /device:TPU:17 now
where the time goes in v2:
time: 140 us; the launch traced here: 139 us
  Pallas kernels  136 us (97%)
  local copies, waits for them, and re-layouts  3.08 us (2%)
    pallas_call x1, Pallas kernels, shared_body(): pl.pallas_call(shared_kernel, out_shape=jax.ShapeDtypeStruct((height, wid...  136 us
    unnamed x1, local copies, waits for them, and re-layouts  3.08 us

profile of v2, /device:TPU:17, one launch (start us, length us, event | category | flops | bytes accessed | tf_op | source)
XLA Modules:
  0.0 139.4 jit_solution(9703523511718182000)
XLA Ops:
  0.0 136.3 %shard_map.28 = f32[1024,512]{1,0:T(8,128)} custom-call(f32[1024,512]{1,0:T(8,128)} %a_in.1, f32[1024,512]{1,0:T(8,128)} %b_in.1), custom_call_target="tpu_custom_call" | custom-call | tf_op jit(solution)/shard_map/pallas_call | solution.py:498
  136.3 3.1 %copy.4 = f32[1024,512]{1,0:T(8,128)} copy(f32[1024,512]{1,0:T(8,128)} %shard_map.28) | data formatting | bytes 4194304
